TPU v7x, 512 devices: a whole 4x8x8 slice. The times are simulated.
512 devices in a mesh: row: 16 (over x, y_lo), col: 32 (over y_hi, z, core).
Axes of the slice: x: 4, y: 8 (y_hi: 2, y_lo: 4; y = y_hi * 4 + y_lo), z: 8, core: 2. Of those that a mesh axis runs over, the one named last changes fastest.
Arguments:
- queries: bfloat16 [2048, 4096], P(('row', 'col')), may hold values from -4 to 4
- documents: bfloat16 [4096, 4096], P(('row', 'col')), may hold values from -4 to 4
- positive: int32 [2048], P(('row', 'col')), may hold values from 0 to 4095, as said below
Outputs:
- mean_loss: float32 [], replicated
- query_grad: bfloat16 [2048, 4096], P(('row', 'col'))
- document_grad: bfloat16 [4096, 4096], P(('row', 'col'))
Inputs may be any that keep to these rules, and one draw needn't show every extreme that they name: `positive`: the 2048 entries are distinct document indices.
All inputs are finite; a program needn't handle non-finite values.
Results may differ from a plain program's by a relative error of at most 0.02.
Values may be sent and summed in bfloat16 or wider, within the bound.
A program may use at most 64 MiB of HBM per device.

v0:
```python
import functools
import math

import jax
import jax.numpy as jnp
from jax import lax
from jax.experimental import pallas as pl
from jax.experimental.pallas import tpu as pltpu
from jax.sharding import PartitionSpec as P

MESH = pl.DeviceIdType.MESH
LEVELS = 4
X, YL, YH, Z = 4, 4, 2, 8
Y = YL * YH
QD, DD = 4, 8
CHUNKS = 2
NEAR = (1, 7, 2, 6, 3, 5, 4)
BF, F32 = jnp.bfloat16, jnp.float32


def wide(value):
    return value.astype(F32)


def kernel(
    q_ref, d_ref, p_ref, loss_ref, dq_ref, dd_ref,
    qbuf, pbuf, dbuf, qdense, pq, pd, sy, sx,
    xr1, xs2, xr2, yp, yr, ys, dsib, zp, zr, zs, lz, lk, dqv, ddv, sems, local,
):
    width = q_ref.shape[1]
    half, quarter = width // 2, width // (2 * CHUNKS)
    row = lax.axis_index("row")
    col = lax.axis_index("col")
    x = row // YL
    y = (col // (Z * 2)) * YL + row % YL
    z = (col // 2) % Z
    k = col % 2

    def at(ax, ay, az, ak):
        return (ax * YL + ay % YL, (ay // YL) * (Z * 2) + az * 2 + ak)

    def yo(o):
        return at(x, (y + o) % Y, z, k)

    def xo(o):
        return at((x + o) % X, y, z, k)

    def zo(o):
        return at(x, y, (z + o) % Z, k)

    sib = at(x, y, z, 1 - k)
    right, left, across = (x + 1) % X, (x + 3) % X, (x + 2) % X
    lo, hi = pl.ds(0, half), pl.ds(half, half)
    started = []

    def send(src, dst, dev):
        n = 2 * len(started)
        copy = pltpu.make_async_remote_copy(
            src_ref=src, dst_ref=dst, send_sem=sems.at[n], recv_sem=sems.at[n + 1],
            device_id=dev, device_id_type=MESH,
        )
        copy.start()
        started.append(copy)
        return copy

    load_q = pltpu.make_async_copy(q_ref, qbuf.at[x, y], local.at[0])
    load_d = pltpu.make_async_copy(d_ref, dbuf.at[k, z], local.at[1])
    load_q.start()
    load_d.start()
    barrier = pltpu.get_barrier_semaphore()
    peers = [zo(o) for o in NEAR] + [yo(o) for o in NEAR] + [xo(o) for o in (1, 3, 2)] + [sib]
    for dev in peers:
        pl.semaphore_signal(barrier, inc=1, device_id=dev, device_id_type=MESH)
    lanes = lax.broadcasted_iota(jnp.int32, (1, X * Y * QD), 1)
    spread = jnp.zeros_like(lanes)
    for i in range(QD):
        spread = jnp.where(lanes % QD == i, p_ref[i], spread)
    pbuf[x, y] = spread
    load_q.wait()
    load_d.wait()
    pl.semaphore_wait(barrier, len(peers))

    qy, qx, qh, dz, dk = {}, {}, {}, {}, {}

    def x_sends(o):
        block = qbuf.at[x, (y + Y - o) % Y]
        qx[o, 0] = send(block, block, xo(1))
        qx[o, 1] = send(block, block, xo(3))

    def x_relay(o):
        yy = (y + Y - o) % Y
        qx[o, 0].wait_recv()
        part = qbuf.at[left, yy, :, lo]
        qh[o, 0] = send(part, part, xo(1))
        qx[o, 1].wait_recv()
        part = qbuf.at[right, yy, :, hi]
        qh[o, 1] = send(part, part, xo(3))

    def y_take(o):
        if o == 4:
            qy[4, 0].wait_recv()
            qy[4, 1].wait_recv()
        else:
            qy[o].wait_recv()
        if o in (2, 6):
            yy = (y + Y - o) % Y
            block = qbuf.at[x, yy]
            near, far, piece = (1, 2, lo) if o == 2 else (7, 6, hi)
            qy[o + near - 8 * (o == 6)] = send(block, block, yo(near))
            part = qbuf.at[x, yy, :, piece]
            qy[4, int(o == 6)] = send(part, part, yo(far))
        x_sends(o)

    def z_take(o):
        if o == 4:
            dz[4, 0].wait_recv()
            dz[4, 1].wait_recv()
        else:
            dz[o].wait_recv()
        zz = (z + Z - o) % Z
        block = dbuf.at[k, zz]
        if o in (2, 6):
            near, far, piece = (1, 2, lo) if o == 2 else (7, 6, hi)
            dz[o + near - 8 * (o == 6)] = send(block, block, zo(near))
            part = dbuf.at[k, zz, :, piece]
            dz[4, int(o == 6)] = send(part, part, zo(far))
        dk[o] = send(block, block, sib)

    own = qbuf.at[x, y]
    for o in (2, 6, 1, 7):
        qy[o] = send(own, own, yo(o))
    x_sends(0)
    own = dbuf.at[k, z]
    for o in (2, 6, 1, 7):
        dz[o] = send(own, own, zo(o))
    pos_y = [send(pbuf.at[x, y], pbuf.at[x, y], yo(o)) for o in NEAR]
    dk[0] = send(own, own, sib)

    y_take(2)
    y_take(6)
    y_take(1)
    y_take(7)
    x_relay(0)
    z_take(2)
    z_take(6)
    y_take(3)
    y_take(5)
    y_take(4)
    x_relay(2)
    x_relay(6)
    z_take(1)
    z_take(7)
    x_relay(1)
    x_relay(7)
    for copy in pos_y:
        copy.wait_recv()
    pos_x = [send(pbuf.at[x], pbuf.at[x], xo(o)) for o in (1, 3, 2)]
    z_take(3)
    z_take(5)
    x_relay(3)
    x_relay(5)
    z_take(4)
    x_relay(4)
    for copy in pos_x:
        copy.wait_recv()
    for copy in dk.values():
        copy.wait_recv()
    for copy in qh.values():
        copy.wait_recv()

    step = min(512, width // 8)
    n_doc = 2 * Z * DD
    n_query = X * Y * QD
    for c in range(0, width, step):
        cs = pl.ds(c, step)
        for a in range(X):
            rows = [wide(qbuf[a, b, :, cs]) for b in range(Y)]
            qdense[a, :, cs] = jnp.concatenate(rows, axis=0).astype(BF)
    pos = jnp.zeros((1, n_query), jnp.int32)
    for a in range(X):
        for b in range(Y):
            pos = pos + jnp.where(lanes // QD == a * Y + b, pbuf[a, b], 0)
    subl = lax.broadcasted_iota(jnp.int32, (n_doc, n_query), 0)
    doc_id = (row * 2 * YH * Z + (col // (Z * 2)) * 2 * Z) * DD
    doc_id = doc_id + (subl // DD % Z) * 2 * DD + (subl // (DD * Z)) * DD + subl % DD
    onehot = jnp.where(doc_id == pos, 1.0, 0.0).astype(F32)

    edges = [0] + [width >> m for m in (3, 2, 1, 0)]
    logits = [None] * LEVELS
    running = None
    for s in range(LEVELS):
        first, end = edges[s], edges[s + 1]
        dpart = dbuf[:, :, :, first:end].reshape(n_doc, end - first)
        qpart = qdense[:, :, first:end].reshape(n_query, end - first)
        dots = lax.dot_general(
            dpart, qpart, (((1,), (1,)), ((), ())), preferred_element_type=F32
        )
        running = dots if running is None else running + dots
        logits[LEVELS - 1 - s] = running * (4.0 / math.sqrt(end))
    picked = jnp.zeros((1, n_query), F32)
    for m in range(LEVELS):
        largest = jnp.max(logits[m], axis=0, keepdims=True)
        sy[0, m : m + 1, :] = largest
        sy[0, LEVELS + m : LEVELS + m + 1, :] = jnp.sum(
            jnp.exp(logits[m] - largest), axis=0, keepdims=True
        )
        picked = picked + jnp.sum(onehot * logits[m], axis=0, keepdims=True)
    sy[0, 2 * LEVELS : 2 * LEVELS + 1, :] = picked

    def merged(ref, n):
        tops = [ref[i, 0:LEVELS, :] for i in range(n)]
        top = functools.reduce(jnp.maximum, tops)
        total = sum(ref[i, LEVELS : 2 * LEVELS, :] * jnp.exp(tops[i] - top) for i in range(n))
        return top, total, sum(ref[i, 2 * LEVELS : 2 * LEVELS + 1, :] for i in range(n))

    stats = [send(sy.at[0], sy.at[o], yo(o)) for o in NEAR]
    for copy in stats:
        copy.wait_recv()
    top, total, picked = merged(sy, Y)
    sx[0, 0:LEVELS, :] = top
    sx[0, LEVELS : 2 * LEVELS, :] = total
    sx[0, 2 * LEVELS : 2 * LEVELS + 1, :] = picked
    stats = [send(sx.at[0], sx.at[o], xo(o)) for o in (1, 3, 2)]
    for copy in stats:
        copy.wait_recv()
    top, total, picked = merged(sx, X)
    lse = top + jnp.log(total)

    grads = []
    weighted = None
    for m in range(LEVELS):
        grad = (jnp.exp(logits[m] - lse[m : m + 1, :]) - onehot) * math.sqrt(2.0**m)
        weighted = grad if weighted is None else weighted + grad
        grads.append(weighted)
    for s in range(LEVELS):
        first, end = edges[s], edges[s + 1]
        g = grads[LEVELS - 1 - s]
        gd = g.astype(BF)
        gq = g.T.astype(BF)
        for c in range(first, end, step):
            cs = pl.ds(c, step)
            part = jnp.dot(gd, qdense[:, :, cs].reshape(n_query, step), preferred_element_type=F32)
            pd[:, :, cs] = part.astype(BF).reshape(2, Z * DD, step)
            part = jnp.dot(gq, dbuf[:, :, :, cs].reshape(n_doc, step), preferred_element_type=F32)
            pq[:, :, cs] = part.astype(BF).reshape(X, Y * QD, step)

    def scatter_start(mine, into, dev):
        return {
            "a": send(mine(3), into(0), dev(1)),
            "A": send(mine(5), into(1), dev(7)),
            "b": send(mine(4, lo_of), into(2, lo_of), dev(2)),
            "B": send(mine(4, hi_of), into(2, hi_of), dev(6)),
            "c": send(mine(1), into(3), dev(1)),
            "C": send(mine(7), into(4), dev(7)),
        }

    def lo_of(n):
        return pl.ds(0, n // 2)

    def hi_of(n):
        return pl.ds(n // 2, n // 2)

    to_sib = send(pd.at[1 - k], dsib, sib)
    x_first, x_direct, x_relayed = {}, {}, {}

    def cols(side, c):
        return pl.ds(side * half + c * quarter, quarter)

    def x_start(c):
        x_first[c, 0] = send(pq.at[across, :, cols(0, c)], xr1.at[c, 0], xo(1))
        x_first[c, 1] = send(pq.at[across, :, cols(1, c)], xr1.at[c, 1], xo(3))

    def x_plain(c):
        x_direct[c, 0] = send(pq.at[right, :, cols(1, c)], xr2.at[c, 1], xo(1))
        x_direct[c, 1] = send(pq.at[left, :, cols(0, c)], xr2.at[c, 2], xo(3))

    def x_pass(c):
        for side, (via, slot, dev) in enumerate(((right, 0, xo(1)), (left, 3, xo(3)))):
            x_first[c, side].wait_recv()
            xs2[c, side] = (wide(pq[via, :, cols(side, c)]) + wide(xr1[c, side])).astype(BF)
            x_relayed[c, side] = send(xs2.at[c, side], xr2.at[c, slot], dev)

    def x_finish(c):
        for side in (0, 1):
            x_relayed[c, side].wait_recv()
            x_direct[c, side].wait_recv()
        for side in (0, 1):
            total = wide(pq[x, :, cols(side, c)]) + wide(xr2[c, side]) + wide(xr2[c, 2 + side])
            for b in range(Y):
                yp[c, b, :, side * quarter : (side + 1) * quarter] = total[
                    b * QD : (b + 1) * QD, :
                ].astype(BF)

    def y_start(c):
        def mine(o, part=None):
            ref = yp.at[c, (y + o) % Y]
            return ref if part is None else yp.at[c, (y + o) % Y, :, part(half)]

        def into(i, part=None):
            return yr.at[c, i] if part is None else yr.at[c, i, :, part(half)]

        return scatter_start(mine, into, yo)

    def y_pass(c, got):
        for side, names in enumerate(("ab", "AB")):
            for name in names:
                got[name].wait_recv()
            own = yp[c, (y + (2, 6)[side]) % Y]
            ys[c, side] = (wide(own) + wide(yr[c, side])).astype(BF)
            part = (lo_of, hi_of)[side](half)
            ys[c, side, :, part] = (
                wide(yp[c, (y + (2, 6)[side]) % Y, :, part])
                + wide(yr[c, side, :, part])
                + wide(yr[c, 2, :, part])
            ).astype(BF)
            got["dD"[side]] = send(ys.at[c, side], yr.at[c, 5 + side], yo((2, 6)[side]))

    for c in range(CHUNKS):
        x_start(c)
    x_plain(0)

    lz[0] = jnp.sum(lse, axis=0, keepdims=True) - picked
    losses = [send(lz.at[0], lz.at[o], zo(o)) for o in NEAR]

    to_sib.wait_recv()
    for b in range(Z):
        rows = slice(b * DD, (b + 1) * DD)
        zp[b] = (wide(pd[k, rows, :]) + wide(dsib[rows, :])).astype(BF)

    def z_mine(o, part=None):
        return zp.at[(z + o) % Z] if part is None else zp.at[(z + o) % Z, :, part(width)]

    def z_into(i, part=None):
        return zr.at[i] if part is None else zr.at[i, :, part(width)]

    zgot = scatter_start(z_mine, z_into, zo)
    x_pass(0)
    for c in range(1, CHUNKS):
        x_plain(c)
        x_pass(c)
    x_finish(0)
    ygot = {0: y_start(0)}
    for side, names in enumerate(("ab", "AB")):
        for name in names:
            zgot[name].wait_recv()
        zz = (z + (2, 6)[side]) % Z
        zs[side] = (wide(zp[zz]) + wide(zr[side])).astype(BF)
        part = (lo_of, hi_of)[side](width)
        zs[side, :, part] = (
            wide(zp[zz, :, part]) + wide(zr[side, :, part]) + wide(zr[2, :, part])
        ).astype(BF)
        zgot["dD"[side]] = send(zs.at[side], zr.at[5 + side], zo((2, 6)[side]))
    for c in range(1, CHUNKS):
        x_finish(c)
        ygot[c] = y_start(c)
    y_pass(0, ygot[0])
    for c in range(1, CHUNKS):
        y_pass(c, ygot[c])

    for copy in losses:
        copy.wait_recv()
    lk[0] = sum(lz[i] for i in range(Z))
    last = send(lk.at[0], lk.at[1], sib)
    for name in "cCdD":
        zgot[name].wait_recv()
    ddv[...] = (
        wide(zp[z]) + wide(zr[3]) + wide(zr[4]) + wide(zr[5]) + wide(zr[6])
    ).astype(BF)
    put_d = pltpu.make_async_copy(ddv, dd_ref, local.at[0])
    put_d.start()
    last.wait_recv()
    scale = 1.0 / (n_query * 2 * Z * LEVELS)
    loss_ref[...] = jnp.sum(lk[0] + lk[1], axis=1, keepdims=True) * scale
    for c in range(CHUNKS):
        for name in "cCdD":
            ygot[c][name].wait_recv()
        total = wide(yp[c, y]) + wide(yr[c, 3]) + wide(yr[c, 4]) + wide(yr[c, 5]) + wide(yr[c, 6])
        for side in (0, 1):
            dqv[:, cols(side, c)] = total[:, side * quarter : (side + 1) * quarter].astype(BF)
    put_q = pltpu.make_async_copy(dqv, dq_ref, local.at[1])
    put_q.start()
    for copy in started:
        copy.wait_send()
    put_d.wait()
    put_q.wait()


def shards(queries, documents, positive):
    width = queries.shape[1]
    half, quarter = width // 2, width // (2 * CHUNKS)
    n_query = X * Y * QD
    vm, dma = pltpu.VMEM, pltpu.SemaphoreType.DMA
    stat = 2 * LEVELS + 1
    anywhere = pl.BlockSpec(memory_space=pl.ANY)
    loss, dq, dd = pl.pallas_call(
        kernel,
        out_shape=[
            jax.ShapeDtypeStruct((1, 1), F32),
            jax.ShapeDtypeStruct(queries.shape, BF),
            jax.ShapeDtypeStruct(documents.shape, BF),
        ],
        in_specs=[anywhere, anywhere, pl.BlockSpec(memory_space=pltpu.SMEM)],
        out_specs=[pl.BlockSpec(memory_space=vm), anywhere, anywhere],
        scratch_shapes=[
            vm((X, Y, QD, width), BF),
            vm((X, Y, 1, n_query), jnp.int32),
            vm((2, Z, DD, width), BF),
            vm((X, Y * QD, width), BF),
            vm((X, Y * QD, width), BF),
            vm((2, Z * DD, width), BF),
            vm((Y, stat, n_query), F32),
            vm((X, stat, n_query), F32),
            vm((CHUNKS, 2, Y * QD, quarter), BF),
            vm((CHUNKS, 2, Y * QD, quarter), BF),
            vm((CHUNKS, 4, Y * QD, quarter), BF),
            vm((CHUNKS, Y, QD, half), BF),
            vm((CHUNKS, 7, QD, half), BF),
            vm((CHUNKS, 2, QD, half), BF),
            vm((Z * DD, width), BF),
            vm((Z, DD, width), BF),
            vm((7, DD, width), BF),
            vm((2, DD, width), BF),
            vm((Z, 1, n_query), F32),
            vm((2, 1, n_query), F32),
            vm(queries.shape, BF),
            vm(documents.shape, BF),
            dma((320,)),
            dma((2,)),
        ],
        compiler_params=pltpu.CompilerParams(collective_id=0, has_side_effects=True),
    )(queries, documents, positive)
    return (loss.reshape(()), dq, dd)


def solution(mesh):
    placed = (P(("row", "col"), None), P(("row", "col"), None), P(("row", "col")))
    return jax.shard_map(
        shards,
        mesh=mesh,
        in_specs=placed,
        out_specs=(P(), P(("row", "col"), None), P(("row", "col"), None)),
        check_vma=False,
    )
```

profile of v0, /device:TPU:1, one launch (start us, length us, event | category | flops | bytes accessed | tf_op | source)
XLA Modules:
  0.0 63.3 jit_solution(13189962890726530109)
XLA Ops:
  0.6 58.9 %shard_map.58 = (f32[1,1]{1,0:T(1,128)}, bf16[4,4096]{1,0:T(4,128)(2,1)}, bf16[8,4096]{1,0:T(8,128)(2,1)}) custom-call(bf16[4,4096]{1,0:T(4,128)(2,1)} %q_ref.1, bf16[8,4096]{1,0:T(8,128)(2,1)} %d_ref.1, s32[4]{0:T(128)} %p_ref.1), custom_call_target="tpu_custom_call" | custom-call | tf_op jit(solution)/shard_map/pallas_call | solution.py:395
  59.5 0.0 copy-start
  60.1 1.4 %copy.10 = bf16[4,4096]{1,0:T(4,128)(2,1)} copy(bf16[4,4096]{1,0:T(4,128)(2,1)} %get-tuple-element.13) | data formatting | bytes 65536
  61.5 0.0 copy-done
  61.5 0.6 copy.11
Async XLA Ops:
  59.5 2.0 %copy-start = (bf16[8,4096]{1,0:T(8,128)(2,1)S(1)}, bf16[8,4096]{1,0:T(8,128)(2,1)}, u32[]{:S(2)}) copy-start(bf16[8,4096]{1,0:T(8,128)(2,1)} %get-tuple-element.14) | copy-start | bytes 196612
where the time goes:
time: 64.1 us; the launch traced here: 63.3 us
  Pallas kernels  58.9 us (92%)
  between operations  2.37 us (4%)
  local copies, waits for them, and re-layouts  2.02 us (3%)
    pallas_call x1, Pallas kernels, shards(): pl.pallas_call(kernel, out_shape=[jax.ShapeDtypeStruct((1, 1), F32), jax....  58.9 us
    unnamed x4, local copies, waits for them, and re-layouts  2.02 us

commit v1 on v0

v1 whole, which is shorter than its diff:
```python
import functools
import math

import jax
import jax.numpy as jnp
from jax import lax
from jax.experimental import pallas as pl
from jax.experimental.pallas import tpu as pltpu
from jax.sharding import PartitionSpec as P

MESH = pl.DeviceIdType.MESH
LEVELS = 4
X, YL, YH, Z = 4, 4, 2, 8
Y = YL * YH
QD, DD = 4, 8
CHUNKS = 2
ALT = 4
NEAR = (1, 7, 2, 6, 3, 5, 4)
BF, F32 = jnp.bfloat16, jnp.float32


def wide(value):
    return value.astype(F32)


def kernel(
    q_ref, d_ref, p_ref, loss_ref, dq_ref, dd_ref,
    qbuf, qalt, pbuf, dbuf, qdense, pq, pqa, pd, sy, sx,
    xr1, xs2, xr2, yp, yr, ys, ayr, ays, axp, axr, dsib, zp, zr, zs, lz, lk,
    lossv, dqv, ddv, psm, bulk, sems, out_sem, local,
):
    width = q_ref.shape[1]
    tail = width // ALT
    main = width - tail
    half, quarter = main // 2, main // (2 * CHUNKS)
    row = lax.axis_index("row")
    col = lax.axis_index("col")
    x = row // YL
    y = (col // (Z * 2)) * YL + row % YL
    z = (col // 2) % Z
    k = col % 2

    def at(ax, ay, az, ak):
        return (ax * YL + ay % YL, (ay // YL) * (Z * 2) + az * 2 + ak)

    def yo(o):
        return at(x, (y + o) % Y, z, k)

    def xo(o):
        return at((x + o) % X, y, z, k)

    def zo(o):
        return at(x, y, (z + o) % Z, k)

    sib = at(x, y, z, 1 - k)
    right, left, across = (x + 1) % X, (x + 3) % X, (x + 2) % X

    def lo_of(n):
        return pl.ds(0, n // 2)

    def hi_of(n):
        return pl.ds(n // 2, n // 2)

    slots = {}
    moved = []

    def sem_of(name):
        return sems.at[slots.setdefault(name, len(slots))]

    def send(src, dst, dev, name):
        moved.append(math.prod(src.shape) * (2 if src.dtype == BF else 4))
        pltpu.make_async_remote_copy(
            src_ref=src, dst_ref=dst, send_sem=out_sem, recv_sem=sem_of(name),
            device_id=dev, device_id_type=MESH,
        ).start()

    def take(name, ref):
        pltpu.make_async_copy(ref, ref, sem_of(name)).wait()

    def spread_start(own, dev, tag):
        for o in (2, 6, 1, 7):
            send(own, own, dev(o), (tag, o))

    def spread_take(o, block, part, dev, tag, n):
        if o == 4:
            take((tag, 4, 0), part(lo_of(n)))
            take((tag, 4, 1), part(hi_of(n)))
        else:
            take((tag, o), block)
        if o == 2:
            send(block, block, dev(1), (tag, 3))
            send(part(lo_of(n)), part(lo_of(n)), dev(2), (tag, 4, 0))
        if o == 6:
            send(block, block, dev(7), (tag, 5))
            send(part(hi_of(n)), part(hi_of(n)), dev(6), (tag, 4, 1))

    def scatter_start(mine, into, dev, tag):
        send(mine(3), into(0), dev(1), (tag, "a"))
        send(mine(5), into(1), dev(7), (tag, "A"))
        send(mine(4, lo_of), into(2, lo_of), dev(2), (tag, "b"))
        send(mine(4, hi_of), into(2, hi_of), dev(6), (tag, "B"))
        send(mine(1), into(3), dev(1), (tag, "c"))
        send(mine(7), into(4), dev(7), (tag, "c"))

    def scatter_pass(mine, into, through, dev, tag):
        for side, part in enumerate((lo_of, hi_of)):
            take((tag, "aA"[side]), into(side))
            take((tag, "bB"[side]), into(2, part))
            via = mine((2, 6)[side])
            out = through(side)
            out[...] = (wide(via[...]) + wide(into(side)[...])).astype(BF)
            piece = through(side, part)
            piece[...] = (
                wide(mine((2, 6)[side], part)[...])
                + wide(into(side, part)[...])
                + wide(into(2, part)[...])
            ).astype(BF)
            send(out, into(5 + side), dev((2, 6)[side]), (tag, "c"))

    loads = [
        pltpu.make_async_copy(q_ref.at[:, pl.ds(0, main)], qbuf.at[x, y], local.at[0]),
        pltpu.make_async_copy(q_ref.at[:, pl.ds(main, tail)], qalt.at[y, x], local.at[1]),
        pltpu.make_async_copy(d_ref, dbuf.at[k, z], local.at[2]),
    ]
    for copy in loads:
        copy.start()
    barrier = pltpu.get_barrier_semaphore()
    peers = [zo(o) for o in NEAR] + [yo(o) for o in NEAR] + [xo(o) for o in (1, 3, 2)] + [sib]
    for dev in peers:
        pl.semaphore_signal(barrier, inc=1, device_id=dev, device_id_type=MESH)
    lanes = lax.broadcasted_iota(jnp.int32, (1, X * Y * QD), 1)
    spread = jnp.zeros_like(lanes)
    for i in range(QD):
        spread = jnp.where(lanes % QD == i, p_ref[i], spread)
    pbuf[x, y] = spread
    for copy in loads:
        copy.wait()
    pl.semaphore_wait(barrier, len(peers))

    def qy_part(yy):
        return lambda cols=None: qbuf.at[x, yy] if cols is None else qbuf.at[x, yy, :, cols]

    def qa_part(yy):
        return lambda cols=None: qalt.at[yy] if cols is None else qalt.at[yy, :, :, cols]

    def dz_part(zz):
        return lambda cols=None: dbuf.at[k, zz] if cols is None else dbuf.at[k, zz, :, cols]

    def x_sends(o):
        block = qbuf.at[x, (y + Y - o) % Y]
        send(block, block, xo(1), ("qx", o, 0))
        send(block, block, xo(3), ("qx", o, 1))

    def x_relay(o):
        yy = (y + Y - o) % Y
        take(("qx", o, 0), qbuf.at[left, yy])
        part = qbuf.at[left, yy, :, lo_of(main)]
        send(part, part, xo(1), "qh")
        take(("qx", o, 1), qbuf.at[right, yy])
        part = qbuf.at[right, yy, :, hi_of(main)]
        send(part, part, xo(3), "qh")

    def y_take(o):
        yy = (y + Y - o) % Y
        spread_take(o, qbuf.at[x, yy], qy_part(yy), yo, "qy", main)
        x_sends(o)

    def a_take(o):
        yy = (y + Y - o) % Y
        spread_take(o, qalt.at[yy], qa_part(yy), yo, "qa", tail)

    def z_take(o):
        zz = (z + Z - o) % Z
        spread_take(o, dbuf.at[k, zz], dz_part(zz), zo, "dz", width)
        send(dbuf.at[k, zz], dbuf.at[k, zz], sib, "dk")

    spread_start(qbuf.at[x, y], yo, "qy")
    for o in (2, 1, 3):
        send(qalt.at[y, x], qalt.at[y, x], xo(o), "qax")
    x_sends(0)
    spread_start(dbuf.at[k, z], zo, "dz")
    for o in NEAR:
        send(pbuf.at[x, y], pbuf.at[x, y], yo(o), "py")
    send(dbuf.at[k, z], dbuf.at[k, z], sib, "dk")

    take("qax", qalt.at[0, pl.ds(0, X - 1)])
    spread_start(qalt.at[y], yo, "qa")
    y_take(2)
    y_take(6)
    y_take(1)
    y_take(7)
    x_relay(0)
    z_take(2)
    z_take(6)
    y_take(3)
    y_take(5)
    a_take(2)
    a_take(6)
    y_take(4)
    x_relay(2)
    x_relay(6)
    take("py", pbuf.at[0, pl.ds(0, Y - 1)])
    for o in (1, 3, 2):
        send(pbuf.at[x], pbuf.at[x], xo(o), "px")
    x_relay(1)
    x_relay(7)
    z_take(1)
    z_take(7)
    x_relay(3)
    x_relay(5)
    z_take(3)
    z_take(5)
    x_relay(4)
    z_take(4)
    for o in (1, 7, 3, 5, 4):
        a_take(o)
    take("px", pbuf.at[pl.ds(0, X - 1)])
    take("qh", qbuf.at[0])
    take("dk", dbuf.at[0])

    step = min(512, width // 8)
    n_doc = 2 * Z * DD
    n_query = X * Y * QD
    for c in range(0, width, step):
        cs = pl.ds(c, step)
        for a in range(X):
            if c < main:
                rows = [wide(qbuf[a, b, :, cs]) for b in range(Y)]
            else:
                rows = [wide(qalt[b, a, :, pl.ds(c - main, step)]) for b in range(Y)]
            qdense[a, :, cs] = jnp.concatenate(rows, axis=0).astype(BF)
    pos = jnp.zeros((1, n_query), jnp.int32)
    for a in range(X):
        for b in range(Y):
            pos = pos + jnp.where(lanes // QD == a * Y + b, pbuf[a, b], 0)
    subl = lax.broadcasted_iota(jnp.int32, (n_doc, n_query), 0)
    doc_id = (row * 2 * YH * Z + (col // (Z * 2)) * 2 * Z) * DD
    doc_id = doc_id + (subl // DD % Z) * 2 * DD + (subl // (DD * Z)) * DD + subl % DD
    onehot = jnp.where(doc_id == pos, 1.0, 0.0).astype(F32)

    edges = [0] + [width >> m for m in (3, 2, 1, 0)]
    logits = [None] * LEVELS
    running = None
    for s in range(LEVELS):
        first, end = edges[s], edges[s + 1]
        dpart = dbuf[:, :, :, first:end].reshape(n_doc, end - first)
        qpart = qdense[:, :, first:end].reshape(n_query, end - first)
        dots = lax.dot_general(
            dpart, qpart, (((1,), (1,)), ((), ())), preferred_element_type=F32
        )
        running = dots if running is None else running + dots
        logits[LEVELS - 1 - s] = running * (4.0 / math.sqrt(end))
    picked = jnp.zeros((1, n_query), F32)
    for m in range(LEVELS):
        largest = jnp.max(logits[m], axis=0, keepdims=True)
        sy[0, m : m + 1, :] = largest
        sy[0, LEVELS + m : LEVELS + m + 1, :] = jnp.sum(
            jnp.exp(logits[m] - largest), axis=0, keepdims=True
        )
        picked = picked + jnp.sum(onehot * logits[m], axis=0, keepdims=True)
    sy[0, 2 * LEVELS : 2 * LEVELS + 1, :] = picked

    def merged(ref, n):
        tops = [ref[i, 0:LEVELS, :] for i in range(n)]
        top = functools.reduce(jnp.maximum, tops)
        total = sum(ref[i, LEVELS : 2 * LEVELS, :] * jnp.exp(tops[i] - top) for i in range(n))
        return top, total, sum(ref[i, 2 * LEVELS : 2 * LEVELS + 1, :] for i in range(n))

    for o in (4, 3, 5, 2, 6, 1, 7):
        send(sy.at[0], sy.at[o], yo(o), "sy")
    take("sy", sy.at[pl.ds(1, Y - 1)])
    top, total, picked = merged(sy, Y)
    sx[0, 0:LEVELS, :] = top
    sx[0, LEVELS : 2 * LEVELS, :] = total
    sx[0, 2 * LEVELS : 2 * LEVELS + 1, :] = picked
    for o in (2, 1, 3):
        send(sx.at[0], sx.at[o], xo(o), "sx")
    take("sx", sx.at[pl.ds(1, X - 1)])
    top, total, picked = merged(sx, X)
    lse = top + jnp.log(total)

    grads = []
    weighted = None
    for m in range(LEVELS):
        grad = (jnp.exp(logits[m] - lse[m : m + 1, :]) - onehot) * math.sqrt(2.0**m)
        weighted = grad if weighted is None else weighted + grad
        grads.append(weighted)
    for s in range(LEVELS):
        first, end = edges[s], edges[s + 1]
        g = grads[LEVELS - 1 - s]
        gd = g.astype(BF)
        gq = g.T.astype(BF)
        for c in range(first, end, step):
            cs = pl.ds(c, step)
            part = jnp.dot(gd, qdense[:, :, cs].reshape(n_query, step), preferred_element_type=F32)
            pd[:, :, cs] = part.astype(BF).reshape(2, Z * DD, step)
            part = jnp.dot(gq, dbuf[:, :, :, cs].reshape(n_doc, step), preferred_element_type=F32)
            if c < main:
                pq[:, :, cs] = part.astype(BF).reshape(X, Y * QD, step)
            else:
                for a in range(X):
                    for b in range(Y):
                        at_row = (a * Y + b) * QD
                        pqa[b, a, :, pl.ds(c - main, step)] = part[at_row : at_row + QD, :].astype(BF)

    def cols(side, c):
        return pl.ds(side * half + c * quarter, quarter)

    def a_mine(o, part=None):
        yy = (y + o) % Y
        return pqa.at[yy] if part is None else pqa.at[yy, :, :, part(tail)]

    def a_into(i, part=None):
        return ayr.at[i] if part is None else ayr.at[i, :, :, part(tail)]

    def a_through(i, part=None):
        return ays.at[i] if part is None else ays.at[i, :, :, part(tail)]

    def x_start(c):
        send(pq.at[across, :, cols(0, c)], xr1.at[c, 0], xo(1), ("xa", c, 0))
        send(pq.at[across, :, cols(1, c)], xr1.at[c, 1], xo(3), ("xa", c, 1))

    def x_plain(c):
        send(pq.at[right, :, cols(1, c)], xr2.at[c, 1], xo(1), ("xc", c))
        send(pq.at[left, :, cols(0, c)], xr2.at[c, 2], xo(3), ("xc", c))

    def x_pass(c):
        for side, (via, slot, dev) in enumerate(((right, 0, xo(1)), (left, 3, xo(3)))):
            take(("xa", c, side), xr1.at[c, side])
            xs2[c, side] = (wide(pq[via, :, cols(side, c)]) + wide(xr1[c, side])).astype(BF)
            send(xs2.at[c, side], xr2.at[c, slot], dev, ("xc", c))

    def y_refs(c):
        def mine(o, part=None):
            yy = (y + o) % Y
            return yp.at[c, yy] if part is None else yp.at[c, yy, :, part(half)]

        def into(i, part=None):
            return yr.at[c, i] if part is None else yr.at[c, i, :, part(half)]

        def through(i, part=None):
            return ys.at[c, i] if part is None else ys.at[c, i, :, part(half)]

        return mine, into, through

    def x_finish(c):
        take(("xc", c), xr2.at[c])
        for side in (0, 1):
            total = wide(pq[x, :, cols(side, c)]) + wide(xr2[c, side]) + wide(xr2[c, 2 + side])
            for b in range(Y):
                yp[c, b, :, side * quarter : (side + 1) * quarter] = total[
                    b * QD : (b + 1) * QD, :
                ].astype(BF)
        mine, into, _ = y_refs(c)
        scatter_start(mine, into, yo, ("y", c))

    for c in range(CHUNKS):
        x_start(c)
    scatter_start(a_mine, a_into, yo, "ay")
    send(pd.at[1 - k], dsib, sib, "sib")
    x_plain(0)

    lz[0] = jnp.sum(lse, axis=0, keepdims=True) - picked
    for o in NEAR:
        send(lz.at[0], lz.at[o], zo(o), "lz")

    take("sib", dsib)
    for b in range(Z):
        rows = slice(b * DD, (b + 1) * DD)
        zp[b] = (wide(pd[k, rows, :]) + wide(dsib[rows, :])).astype(BF)

    def z_mine(o, part=None):
        zz = (z + o) % Z
        return zp.at[zz] if part is None else zp.at[zz, :, part(width)]

    def z_into(i, part=None):
        return zr.at[i] if part is None else zr.at[i, :, part(width)]

    def z_through(i, part=None):
        return zs.at[i] if part is None else zs.at[i, :, part(width)]

    scatter_start(z_mine, z_into, zo, "z")
    x_pass(0)
    for c in range(1, CHUNKS):
        x_plain(c)
        x_pass(c)
    scatter_pass(a_mine, a_into, a_through, yo, "ay")
    x_finish(0)
    scatter_pass(z_mine, z_into, z_through, zo, "z")
    take(("ay", "c"), ayr.at[pl.ds(3, 4)])
    for a in range(X):
        total = wide(pqa[y, a])
        for i in (3, 4, 5, 6):
            total = total + wide(ayr[i, a])
        axp[a] = total.astype(BF)
    for o in (2, 1, 3):
        send(axp.at[(x + o) % X], axr.at[o], xo(o), "ax")
    for c in range(1, CHUNKS):
        x_finish(c)
    take("lz", lz.at[pl.ds(1, Z - 1)])
    lk[0] = sum(lz[i] for i in range(Z))
    send(lk.at[0], lk.at[1], sib, "lk")
    for c in range(CHUNKS):
        scatter_pass(*y_refs(c), yo, ("y", c))
    take("ax", axr.at[pl.ds(1, X - 1)])
    total = wide(axp[x])
    for o in (1, 2, 3):
        total = total + wide(axr[o])
    dqv[:, main:] = total.astype(BF)
    take("lk", lk.at[1])
    scale = 1.0 / (n_query * 2 * Z * LEVELS)
    total = jnp.sum(lk[0] + lk[1], axis=1, keepdims=True) * scale
    lossv[...] = jnp.broadcast_to(total, (1, n_query))
    puts = [pltpu.make_async_copy(lossv, loss_ref, local.at[0])]
    puts[0].start()
    take(("z", "c"), zr.at[pl.ds(3, 4)])
    ddv[...] = (
        wide(zp[z]) + wide(zr[3]) + wide(zr[4]) + wide(zr[5]) + wide(zr[6])
    ).astype(BF)
    puts.append(pltpu.make_async_copy(ddv, dd_ref, local.at[1]))
    puts[1].start()
    for c in range(CHUNKS):
        take((("y", c), "c"), yr.at[c, pl.ds(3, 4)])
        total = wide(yp[c, y]) + wide(yr[c, 3]) + wide(yr[c, 4]) + wide(yr[c, 5]) + wide(yr[c, 6])
        for side in (0, 1):
            dqv[:, cols(side, c)] = total[:, side * quarter : (side + 1) * quarter].astype(BF)
    puts.append(pltpu.make_async_copy(dqv, dq_ref, local.at[2]))
    puts[2].start()
    sent = bulk.at[pl.ds(0, sum(moved) // 512)]
    pltpu.make_async_copy(sent, sent, out_sem).wait()
    for copy in puts:
        copy.wait()


def shards(queries, documents, positive):
    width = queries.shape[1]
    tail = width // ALT
    main = width - tail
    half, quarter = main // 2, main // (2 * CHUNKS)
    n_query = X * Y * QD
    vm, dma = pltpu.VMEM, pltpu.SemaphoreType.DMA
    stat = 2 * LEVELS + 1
    anywhere = pl.BlockSpec(memory_space=pl.ANY)
    loss, dq, dd = pl.pallas_call(
        kernel,
        out_shape=[
            jax.ShapeDtypeStruct((1, n_query), F32),
            jax.ShapeDtypeStruct(queries.shape, BF),
            jax.ShapeDtypeStruct(documents.shape, BF),
        ],
        in_specs=[anywhere, anywhere, pl.BlockSpec(memory_space=pltpu.SMEM)],
        out_specs=[anywhere] * 3,
        scratch_shapes=[
            vm((X, Y, QD, main), BF),
            vm((Y, X, QD, tail), BF),
            vm((X, Y, 1, n_query), jnp.int32),
            vm((2, Z, DD, width), BF),
            vm((X, Y * QD, width), BF),
            vm((X, Y * QD, main), BF),
            vm((Y, X, QD, tail), BF),
            vm((2, Z * DD, width), BF),
            vm((Y, stat, n_query), F32),
            vm((X, stat, n_query), F32),
            vm((CHUNKS, 2, Y * QD, quarter), BF),
            vm((CHUNKS, 2, Y * QD, quarter), BF),
            vm((CHUNKS, 4, Y * QD, quarter), BF),
            vm((CHUNKS, Y, QD, half), BF),
            vm((CHUNKS, 7, QD, half), BF),
            vm((CHUNKS, 2, QD, half), BF),
            vm((7, X, QD, tail), BF),
            vm((2, X, QD, tail), BF),
            vm((X, QD, tail), BF),
            vm((X, QD, tail), BF),
            vm((Z * DD, width), BF),
            vm((Z, DD, width), BF),
            vm((7, DD, width), BF),
            vm((2, DD, width), BF),
            vm((Z, 1, n_query), F32),
            vm((2, 1, n_query), F32),
            vm((1, n_query), F32),
            vm(queries.shape, BF),
            vm(documents.shape, BF),
            pltpu.SMEM((QD,), jnp.int32),
            vm((16384, 128), F32),
            dma((80,)),
            dma,
            dma((3,)),
        ],
        compiler_params=pltpu.CompilerParams(collective_id=0, has_side_effects=True),
    )(queries, documents, positive)
    return (loss[0, 0], dq, dd)


def solution(mesh):
    placed = (P(("row", "col"), None), P(("row", "col"), None), P(("row", "col")))
    return jax.shard_map(
        shards,
        mesh=mesh,
        in_specs=placed,
        out_specs=(P(), P(("row", "col"), None), P(("row", "col"), None)),
        check_vma=False,
    )
```

time: 64.1 us -> 60.5 us (0.944)
  the two profiles are of different devices: /device:TPU:1 before, /device:TPU:16 now
where the time goes in v1:
time: 60.5 us; the launch traced here: 60.2 us
  Pallas kernels  55.9 us (92%)
  between operations  2.37 us (4%)
  local copies, waits for them, and re-layouts  2.02 us (3%)
    pallas_call x1, Pallas kernels, shards(): pl.pallas_call(kernel, out_shape=[jax.ShapeDtypeStruct((1, n_query), F32)...  55.9 us
    unnamed x4, local copies, waits for them, and re-layouts  2.02 us

profile of v1, /device:TPU:16, one launch (start us, length us, event | category | flops | bytes accessed | tf_op | source)
XLA Modules:
  0.0 60.2 jit_solution(8300547153155216525)
XLA Ops:
  0.6 55.9 %shard_map.58 = (f32[1,128]{1,0:T(1,128)}, bf16[4,4096]{1,0:T(4,128)(2,1)}, bf16[8,4096]{1,0:T(8,128)(2,1)}) custom-call(bf16[4,4096]{1,0:T(4,128)(2,1)} %q_ref.1, bf16[8,4096]{1,0:T(8,128)(2,1)} %d_ref.1, s32[4]{0:T(128)} %p_ref.1), custom_call_target="tpu_custom_call" | custom-call | tf_op jit(solution)/shard_map/pallas_call | solution.py:444
  56.5 0.0 copy-start
  57.1 1.4 %copy.10 = bf16[4,4096]{1,0:T(4,128)(2,1)} copy(bf16[4,4096]{1,0:T(4,128)(2,1)} %get-tuple-element.13) | data formatting | bytes 65536
  58.5 0.0 copy-done
  58.5 0.6 %copy.11 = bf16[8,4096]{1,0:T(8,128)(2,1)} copy(bf16[8,4096]{1,0:T(8,128)(2,1)S(1)} %copy-done) | data formatting | bytes 131072
Async XLA Ops:
  56.5 2.0 %copy-start = (bf16[8,4096]{1,0:T(8,128)(2,1)S(1)}, bf16[8,4096]{1,0:T(8,128)(2,1)}, u32[]{:S(2)}) copy-start(bf16[8,4096]{1,0:T(8,128)(2,1)} %get-tuple-element.14) | copy-start | bytes 196612

commit v2 on v1

--- a/solution.py
+++ b/solution.py
@@ -13,8 +13,8 @@
 X, YL, YH, Z = 4, 4, 2, 8
 Y = YL * YH
 QD, DD = 4, 8
-CHUNKS = 2
-ALT = 4
+ALT = 5 / 16
+FAR = (4, 3, 5, 2, 6, 1, 7)
 NEAR = (1, 7, 2, 6, 3, 5, 4)
 BF, F32 = jnp.bfloat16, jnp.float32
 
@@ -26,13 +26,12 @@
 def kernel(
     q_ref, d_ref, p_ref, loss_ref, dq_ref, dd_ref,
     qbuf, qalt, pbuf, dbuf, qdense, pq, pqa, pd, sy, sx,
-    xr1, xs2, xr2, yp, yr, ys, ayr, ays, axp, axr, dsib, zp, zr, zs, lz, lk,
-    lossv, dqv, ddv, psm, bulk, sems, out_sem, local,
+    xr, yp, yr, ayr, ays, axp, axr, dsib, zp, zr, zs, lz, lk,
+    lossv, dqv, ddv, bulk, sems, out_sem, local,
 ):
     width = q_ref.shape[1]
-    tail = width // ALT
+    tail = int(width * ALT)
     main = width - tail
-    half, quarter = main // 2, main // (2 * CHUNKS)
     row = lax.axis_index("row")
     col = lax.axis_index("col")
     x = row // YL
@@ -53,7 +52,6 @@
         return at(x, y, (z + o) % Z, k)
 
     sib = at(x, y, z, 1 - k)
-    right, left, across = (x + 1) % X, (x + 3) % X, (x + 2) % X
 
     def lo_of(n):
         return pl.ds(0, n // 2)
@@ -137,9 +135,6 @@
         copy.wait()
     pl.semaphore_wait(barrier, len(peers))
 
-    def qy_part(yy):
-        return lambda cols=None: qbuf.at[x, yy] if cols is None else qbuf.at[x, yy, :, cols]
-
     def qa_part(yy):
         return lambda cols=None: qalt.at[yy] if cols is None else qalt.at[yy, :, :, cols]
 
@@ -148,21 +143,11 @@
 
     def x_sends(o):
         block = qbuf.at[x, (y + Y - o) % Y]
-        send(block, block, xo(1), ("qx", o, 0))
-        send(block, block, xo(3), ("qx", o, 1))
-
-    def x_relay(o):
-        yy = (y + Y - o) % Y
-        take(("qx", o, 0), qbuf.at[left, yy])
-        part = qbuf.at[left, yy, :, lo_of(main)]
-        send(part, part, xo(1), "qh")
-        take(("qx", o, 1), qbuf.at[right, yy])
-        part = qbuf.at[right, yy, :, hi_of(main)]
-        send(part, part, xo(3), "qh")
+        for dx in (2, 1, 3):
+            send(block, block, xo(dx), "qx")
 
     def y_take(o):
-        yy = (y + Y - o) % Y
-        spread_take(o, qbuf.at[x, yy], qy_part(yy), yo, "qy", main)
+        take(("qy", o), qbuf.at[x, y])
         x_sends(o)
 
     def a_take(o):
@@ -174,7 +159,8 @@
         spread_take(o, dbuf.at[k, zz], dz_part(zz), zo, "dz", width)
         send(dbuf.at[k, zz], dbuf.at[k, zz], sib, "dk")
 
-    spread_start(qbuf.at[x, y], yo, "qy")
+    for o in NEAR:
+        send(qbuf.at[x, y], qbuf.at[x, y], yo(o), ("qy", o))
     for o in (2, 1, 3):
         send(qalt.at[y, x], qalt.at[y, x], xo(o), "qax")
     x_sends(0)
@@ -183,51 +169,45 @@
         send(pbuf.at[x, y], pbuf.at[x, y], yo(o), "py")
     send(dbuf.at[k, z], dbuf.at[k, z], sib, "dk")
 
+    y_take(1)
+    y_take(7)
     take("qax", qalt.at[0, pl.ds(0, X - 1)])
     spread_start(qalt.at[y], yo, "qa")
     y_take(2)
     y_take(6)
-    y_take(1)
-    y_take(7)
-    x_relay(0)
     z_take(2)
     z_take(6)
     y_take(3)
     y_take(5)
+    y_take(4)
     a_take(2)
     a_take(6)
-    y_take(4)
-    x_relay(2)
-    x_relay(6)
     take("py", pbuf.at[0, pl.ds(0, Y - 1)])
     for o in (1, 3, 2):
         send(pbuf.at[x], pbuf.at[x], xo(o), "px")
-    x_relay(1)
-    x_relay(7)
-    z_take(1)
-    z_take(7)
-    x_relay(3)
-    x_relay(5)
-    z_take(3)
-    z_take(5)
-    x_relay(4)
-    z_take(4)
+    for o in (1, 7, 3, 5, 4):
+        z_take(o)
     for o in (1, 7, 3, 5, 4):
         a_take(o)
     take("px", pbuf.at[pl.ds(0, X - 1)])
-    take("qh", qbuf.at[0])
+    take("qx", qbuf.at[pl.ds(0, X - 1)])
     take("dk", dbuf.at[0])
 
     step = min(512, width // 8)
     n_doc = 2 * Z * DD
     n_query = X * Y * QD
-    for c in range(0, width, step):
-        cs = pl.ds(c, step)
+
+    def pieces(first, end):
+        cuts = sorted({*range(first, end, step), end} | ({main} if first < main < end else set()))
+        return [(c, d - c) for c, d in zip(cuts, cuts[1:])]
+
+    for c, n in pieces(0, width):
+        cs = pl.ds(c, n)
         for a in range(X):
             if c < main:
                 rows = [wide(qbuf[a, b, :, cs]) for b in range(Y)]
             else:
-                rows = [wide(qalt[b, a, :, pl.ds(c - main, step)]) for b in range(Y)]
+                rows = [wide(qalt[b, a, :, pl.ds(c - main, n)]) for b in range(Y)]
             qdense[a, :, cs] = jnp.concatenate(rows, axis=0).astype(BF)
     pos = jnp.zeros((1, n_query), jnp.int32)
     for a in range(X):
@@ -290,21 +270,18 @@
         g = grads[LEVELS - 1 - s]
         gd = g.astype(BF)
         gq = g.T.astype(BF)
-        for c in range(first, end, step):
-            cs = pl.ds(c, step)
-            part = jnp.dot(gd, qdense[:, :, cs].reshape(n_query, step), preferred_element_type=F32)
-            pd[:, :, cs] = part.astype(BF).reshape(2, Z * DD, step)
-            part = jnp.dot(gq, dbuf[:, :, :, cs].reshape(n_doc, step), preferred_element_type=F32)
-            if c < main:
-                pq[:, :, cs] = part.astype(BF).reshape(X, Y * QD, step)
-            else:
-                for a in range(X):
-                    for b in range(Y):
-                        at_row = (a * Y + b) * QD
-                        pqa[b, a, :, pl.ds(c - main, step)] = part[at_row : at_row + QD, :].astype(BF)
-
-    def cols(side, c):
-        return pl.ds(side * half + c * quarter, quarter)
+        for c, n in pieces(first, end):
+            part = jnp.dot(gd, qdense[:, :, c : c + n].reshape(n_query, n), preferred_element_type=F32)
+            pd[:, :, c : c + n] = part.astype(BF).reshape(2, Z * DD, n)
+            part = jnp.dot(gq, dbuf[:, :, :, c : c + n].reshape(n_doc, n), preferred_element_type=F32)
+            for a in range(X):
+                for b in range(Y):
+                    at_row = (a * Y + b) * QD
+                    block = part[at_row : at_row + QD, :].astype(BF)
+                    if c < main:
+                        pq[a, b, :, c : c + n] = block
+                    else:
+                        pqa[b, a, :, c - main : c - main + n] = block
 
     def a_mine(o, part=None):
         yy = (y + o) % Y
@@ -316,49 +293,26 @@
     def a_through(i, part=None):
         return ays.at[i] if part is None else ays.at[i, :, :, part(tail)]
 
-    def x_start(c):
-        send(pq.at[across, :, cols(0, c)], xr1.at[c, 0], xo(1), ("xa", c, 0))
-        send(pq.at[across, :, cols(1, c)], xr1.at[c, 1], xo(3), ("xa", c, 1))
-
-    def x_plain(c):
-        send(pq.at[right, :, cols(1, c)], xr2.at[c, 1], xo(1), ("xc", c))
-        send(pq.at[left, :, cols(0, c)], xr2.at[c, 2], xo(3), ("xc", c))
-
-    def x_pass(c):
-        for side, (via, slot, dev) in enumerate(((right, 0, xo(1)), (left, 3, xo(3)))):
-            take(("xa", c, side), xr1.at[c, side])
-            xs2[c, side] = (wide(pq[via, :, cols(side, c)]) + wide(xr1[c, side])).astype(BF)
-            send(xs2.at[c, side], xr2.at[c, slot], dev, ("xc", c))
-
-    def y_refs(c):
-        def mine(o, part=None):
-            yy = (y + o) % Y
-            return yp.at[c, yy] if part is None else yp.at[c, yy, :, part(half)]
-
-        def into(i, part=None):
-            return yr.at[c, i] if part is None else yr.at[c, i, :, part(half)]
-
-        def through(i, part=None):
-            return ys.at[c, i] if part is None else ys.at[c, i, :, part(half)]
-
-        return mine, into, through
-
-    def x_finish(c):
-        take(("xc", c), xr2.at[c])
-        for side in (0, 1):
-            total = wide(pq[x, :, cols(side, c)]) + wide(xr2[c, side]) + wide(xr2[c, 2 + side])
-            for b in range(Y):
-                yp[c, b, :, side * quarter : (side + 1) * quarter] = total[
-                    b * QD : (b + 1) * QD, :
-                ].astype(BF)
-        mine, into, _ = y_refs(c)
-        scatter_start(mine, into, yo, ("y", c))
-
-    for c in range(CHUNKS):
-        x_start(c)
+    def x_start(o):
+        yy = (y + o) % Y
+        for dx in (2, 1, 3):
+            send(pq.at[(x + dx) % X, yy], xr.at[o, dx - 1], xo(dx), ("x", o))
+
+    def x_finish(o):
+        take(("x", o), xr.at[o])
+        total = wide(pq[x, (y + o) % Y])
+        for i in range(X - 1):
+            total = total + wide(xr[o, i])
+        if o:
+            yp[o] = total.astype(BF)
+            send(yp.at[o], yr.at[o], yo(o), "y")
+        return total
+
+    x_start(4)
     scatter_start(a_mine, a_into, yo, "ay")
     send(pd.at[1 - k], dsib, sib, "sib")
-    x_plain(0)
+    for o in FAR[1:] + (0,):
+        x_start(o)
 
     lz[0] = jnp.sum(lse, axis=0, keepdims=True) - picked
     for o in NEAR:
@@ -380,12 +334,12 @@
         return zs.at[i] if part is None else zs.at[i, :, part(width)]
 
     scatter_start(z_mine, z_into, zo, "z")
-    x_pass(0)
-    for c in range(1, CHUNKS):
-        x_plain(c)
-        x_pass(c)
+    x_finish(4)
+    x_finish(3)
+    x_finish(5)
     scatter_pass(a_mine, a_into, a_through, yo, "ay")
-    x_finish(0)
+    x_finish(2)
+    x_finish(6)
     scatter_pass(z_mine, z_into, z_through, zo, "z")
     take(("ay", "c"), ayr.at[pl.ds(3, 4)])
     for a in range(X):
@@ -395,13 +349,11 @@
         axp[a] = total.astype(BF)
     for o in (2, 1, 3):
         send(axp.at[(x + o) % X], axr.at[o], xo(o), "ax")
-    for c in range(1, CHUNKS):
-        x_finish(c)
+    x_finish(1)
+    x_finish(7)
     take("lz", lz.at[pl.ds(1, Z - 1)])
     lk[0] = sum(lz[i] for i in range(Z))
     send(lk.at[0], lk.at[1], sib, "lk")
-    for c in range(CHUNKS):
-        scatter_pass(*y_refs(c), yo, ("y", c))
     take("ax", axr.at[pl.ds(1, X - 1)])
     total = wide(axp[x])
     for o in (1, 2, 3):
@@ -419,11 +371,11 @@
     ).astype(BF)
     puts.append(pltpu.make_async_copy(ddv, dd_ref, local.at[1]))
     puts[1].start()
-    for c in range(CHUNKS):
-        take((("y", c), "c"), yr.at[c, pl.ds(3, 4)])
-        total = wide(yp[c, y]) + wide(yr[c, 3]) + wide(yr[c, 4]) + wide(yr[c, 5]) + wide(yr[c, 6])
-        for side in (0, 1):
-            dqv[:, cols(side, c)] = total[:, side * quarter : (side + 1) * quarter].astype(BF)
+    total = x_finish(0)
+    take("y", yr.at[pl.ds(1, Y - 1)])
+    for o in NEAR:
+        total = total + wide(yr[o])
+    dqv[:, :main] = total.astype(BF)
     puts.append(pltpu.make_async_copy(dqv, dq_ref, local.at[2]))
     puts[2].start()
     sent = bulk.at[pl.ds(0, sum(moved) // 512)]
@@ -434,9 +386,8 @@
 
 def shards(queries, documents, positive):
     width = queries.shape[1]
-    tail = width // ALT
+    tail = int(width * ALT)
     main = width - tail
-    half, quarter = main // 2, main // (2 * CHUNKS)
     n_query = X * Y * QD
     vm, dma = pltpu.VMEM, pltpu.SemaphoreType.DMA
     stat = 2 * LEVELS + 1
@@ -456,17 +407,14 @@
             vm((X, Y, 1, n_query), jnp.int32),
             vm((2, Z, DD, width), BF),
             vm((X, Y * QD, width), BF),
-            vm((X, Y * QD, main), BF),
+            vm((X, Y, QD, main), BF),
             vm((Y, X, QD, tail), BF),
             vm((2, Z * DD, width), BF),
             vm((Y, stat, n_query), F32),
             vm((X, stat, n_query), F32),
-            vm((CHUNKS, 2, Y * QD, quarter), BF),
-            vm((CHUNKS, 2, Y * QD, quarter), BF),
-            vm((CHUNKS, 4, Y * QD, quarter), BF),
-            vm((CHUNKS, Y, QD, half), BF),
-            vm((CHUNKS, 7, QD, half), BF),
-            vm((CHUNKS, 2, QD, half), BF),
+            vm((Y, X - 1, QD, main), BF),
+            vm((Y, QD, main), BF),
+            vm((Y, QD, main), BF),
             vm((7, X, QD, tail), BF),
             vm((2, X, QD, tail), BF),
             vm((X, QD, tail), BF),
@@ -480,9 +428,8 @@
             vm((1, n_query), F32),
             vm(queries.shape, BF),
             vm(documents.shape, BF),
-            pltpu.SMEM((QD,), jnp.int32),
             vm((16384, 128), F32),
-            dma((80,)),
+            dma((54,)),
             dma,
             dma((3,)),
         ],

time: 60.5 us -> 56.2 us (0.929)
  Pallas kernels: 55.9 us -> 51.6 us
    pallas_call x1, Pallas kernels: 55.9 us -> 51.6 us  [shards(): pl.pallas_call(kernel, out_shape=[jax.ShapeDtypeStruct((1, n_query), F32)...]
where the time goes in v2:
time: 56.2 us; the launch traced here: 55.9 us
  Pallas kernels  51.6 us (92%)
  between operations  2.37 us (4%)
  local copies, waits for them, and re-layouts  2.02 us (4%)
    pallas_call x1, Pallas kernels, shards(): pl.pallas_call(kernel, out_shape=[jax.ShapeDtypeStruct((1, n_query), F32)...  51.6 us
    unnamed x4, local copies, waits for them, and re-layouts  2.02 us

profile of v2, /device:TPU:16, one launch (start us, length us, event | category | flops | bytes accessed | tf_op | source)
XLA Modules:
  0.0 55.9 jit_solution(5329182289262368203)
XLA Ops:
  0.6 51.6 %shard_map.58 = (f32[1,128]{1,0:T(1,128)}, bf16[4,4096]{1,0:T(4,128)(2,1)}, bf16[8,4096]{1,0:T(8,128)(2,1)}) custom-call(bf16[4,4096]{1,0:T(4,128)(2,1)} %q_ref.1, bf16[8,4096]{1,0:T(8,128)(2,1)} %d_ref.1, s32[4]{0:T(128)} %p_ref.1), custom_call_target="tpu_custom_call" | custom-call | tf_op jit(solution)/shard_map/pallas_call | solution.py:395
  52.2 0.0 copy-start
  52.8 1.4 %copy.10 = bf16[4,4096]{1,0:T(4,128)(2,1)} copy(bf16[4,4096]{1,0:T(4,128)(2,1)} %get-tuple-element.13) | data formatting | bytes 65536
  54.2 0.0 copy-done
  54.2 0.6 %copy.11 = bf16[8,4096]{1,0:T(8,128)(2,1)} copy(bf16[8,4096]{1,0:T(8,128)(2,1)S(1)} %copy-done) | data formatting | bytes 131072
Async XLA Ops:
  52.2 2.0 %copy-start = (bf16[8,4096]{1,0:T(8,128)(2,1)S(1)}, bf16[8,4096]{1,0:T(8,128)(2,1)}, u32[]{:S(2)}) copy-start(bf16[8,4096]{1,0:T(8,128)(2,1)} %get-tuple-element.14) | copy-start | bytes 196612

commit v3 on v2

--- a/solution.py
+++ b/solution.py
@@ -27,7 +27,7 @@
     q_ref, d_ref, p_ref, loss_ref, dq_ref, dd_ref,
     qbuf, qalt, pbuf, dbuf, qdense, pq, pqa, pd, sy, sx,
     xr, yp, yr, ayr, ays, axp, axr, dsib, zp, zr, zs, lz, lk,
-    lossv, dqv, ddv, bulk, sems, out_sem, local,
+    lossv, dqv, ddv, psm, bulk, sems, out_sem, local,
 ):
     width = q_ref.shape[1]
     tail = int(width * ALT)
@@ -115,6 +115,8 @@
             ).astype(BF)
             send(out, into(5 + side), dev((2, 6)[side]), (tag, "c"))
 
+    load_p = pltpu.make_async_copy(p_ref, psm, local.at[3])
+    load_p.start()
     loads = [
         pltpu.make_async_copy(q_ref.at[:, pl.ds(0, main)], qbuf.at[x, y], local.at[0]),
         pltpu.make_async_copy(q_ref.at[:, pl.ds(main, tail)], qalt.at[y, x], local.at[1]),
@@ -127,10 +129,6 @@
     for dev in peers:
         pl.semaphore_signal(barrier, inc=1, device_id=dev, device_id_type=MESH)
     lanes = lax.broadcasted_iota(jnp.int32, (1, X * Y * QD), 1)
-    spread = jnp.zeros_like(lanes)
-    for i in range(QD):
-        spread = jnp.where(lanes % QD == i, p_ref[i], spread)
-    pbuf[x, y] = spread
     for copy in loads:
         copy.wait()
     pl.semaphore_wait(barrier, len(peers))
@@ -165,6 +163,11 @@
         send(qalt.at[y, x], qalt.at[y, x], xo(o), "qax")
     x_sends(0)
     spread_start(dbuf.at[k, z], zo, "dz")
+    load_p.wait()
+    spread = jnp.zeros_like(lanes)
+    for i in range(QD):
+        spread = jnp.where(lanes % QD == i, psm[i], spread)
+    pbuf[x, y] = spread
     for o in NEAR:
         send(pbuf.at[x, y], pbuf.at[x, y], yo(o), "py")
     send(dbuf.at[k, z], dbuf.at[k, z], sib, "dk")
@@ -187,12 +190,6 @@
         send(pbuf.at[x], pbuf.at[x], xo(o), "px")
     for o in (1, 7, 3, 5, 4):
         z_take(o)
-    for o in (1, 7, 3, 5, 4):
-        a_take(o)
-    take("px", pbuf.at[pl.ds(0, X - 1)])
-    take("qx", qbuf.at[pl.ds(0, X - 1)])
-    take("dk", dbuf.at[0])
-
     step = min(512, width // 8)
     n_doc = 2 * Z * DD
     n_query = X * Y * QD
@@ -201,14 +198,19 @@
         cuts = sorted({*range(first, end, step), end} | ({main} if first < main < end else set()))
         return [(c, d - c) for c, d in zip(cuts, cuts[1:])]
 
-    for c, n in pieces(0, width):
-        cs = pl.ds(c, n)
-        for a in range(X):
-            if c < main:
-                rows = [wide(qbuf[a, b, :, cs]) for b in range(Y)]
-            else:
-                rows = [wide(qalt[b, a, :, pl.ds(c - main, n)]) for b in range(Y)]
-            qdense[a, :, cs] = jnp.concatenate(rows, axis=0).astype(BF)
+    def densify(first, end, block):
+        for c, n in pieces(first, end):
+            for a in range(X):
+                rows = [wide(block(a, b, c, n)) for b in range(Y)]
+                qdense[a, :, c : c + n] = jnp.concatenate(rows, axis=0).astype(BF)
+
+    take("qx", qbuf.at[pl.ds(0, X - 1)])
+    densify(0, main, lambda a, b, c, n: qbuf[a, b, :, c : c + n])
+    for o in (1, 7, 3, 5, 4):
+        a_take(o)
+    densify(main, width, lambda a, b, c, n: qalt[b, a, :, c - main : c - main + n])
+    take("px", pbuf.at[pl.ds(0, X - 1)])
+    take("dk", dbuf.at[0])
     pos = jnp.zeros((1, n_query), jnp.int32)
     for a in range(X):
         for b in range(Y):
@@ -266,13 +268,14 @@
         weighted = grad if weighted is None else weighted + grad
         grads.append(weighted)
     for s in range(LEVELS):
-        first, end = edges[s], edges[s + 1]
-        g = grads[LEVELS - 1 - s]
-        gd = g.astype(BF)
-        gq = g.T.astype(BF)
-        for c, n in pieces(first, end):
+        gd = grads[LEVELS - 1 - s].astype(BF)
+        for c, n in pieces(edges[s], edges[s + 1]):
             part = jnp.dot(gd, qdense[:, :, c : c + n].reshape(n_query, n), preferred_element_type=F32)
             pd[:, :, c : c + n] = part.astype(BF).reshape(2, Z * DD, n)
+    send(pd.at[1 - k], dsib, sib, "sib")
+    for s in range(LEVELS):
+        gq = grads[LEVELS - 1 - s].T.astype(BF)
+        for c, n in pieces(edges[s], edges[s + 1]):
             part = jnp.dot(gq, dbuf[:, :, :, c : c + n].reshape(n_doc, n), preferred_element_type=F32)
             for a in range(X):
                 for b in range(Y):
@@ -310,7 +313,6 @@
 
     x_start(4)
     scatter_start(a_mine, a_into, yo, "ay")
-    send(pd.at[1 - k], dsib, sib, "sib")
     for o in FAR[1:] + (0,):
         x_start(o)
 
@@ -335,12 +337,15 @@
 
     scatter_start(z_mine, z_into, zo, "z")
     x_finish(4)
+    scatter_pass(a_mine, a_into, a_through, yo, "ay")
     x_finish(3)
     x_finish(5)
-    scatter_pass(a_mine, a_into, a_through, yo, "ay")
     x_finish(2)
     x_finish(6)
+    x_finish(1)
+    x_finish(7)
     scatter_pass(z_mine, z_into, z_through, zo, "z")
+    mine = x_finish(0)
     take(("ay", "c"), ayr.at[pl.ds(3, 4)])
     for a in range(X):
         total = wide(pqa[y, a])
@@ -349,8 +354,6 @@
         axp[a] = total.astype(BF)
     for o in (2, 1, 3):
         send(axp.at[(x + o) % X], axr.at[o], xo(o), "ax")
-    x_finish(1)
-    x_finish(7)
     take("lz", lz.at[pl.ds(1, Z - 1)])
     lk[0] = sum(lz[i] for i in range(Z))
     send(lk.at[0], lk.at[1], sib, "lk")
@@ -371,16 +374,31 @@
     ).astype(BF)
     puts.append(pltpu.make_async_copy(ddv, dd_ref, local.at[1]))
     puts[1].start()
-    total = x_finish(0)
     take("y", yr.at[pl.ds(1, Y - 1)])
     for o in NEAR:
-        total = total + wide(yr[o])
-    dqv[:, :main] = total.astype(BF)
+        mine = mine + wide(yr[o])
+    dqv[:, :main] = mine.astype(BF)
     puts.append(pltpu.make_async_copy(dqv, dq_ref, local.at[2]))
     puts[2].start()
     sent = bulk.at[pl.ds(0, sum(moved) // 512)]
     pltpu.make_async_copy(sent, sent, out_sem).wait()
     for copy in puts:
+        copy.wait()
+
+
+def finish(loss_ref, dq_ref, dd_ref, loss_out, dq_out, dd_out, lossv, dqv, ddv, mean, sems):
+    pairs = ((dd_ref, ddv), (dq_ref, dqv), (loss_ref, lossv))
+    ins = [pltpu.make_async_copy(a, b, sems.at[i]) for i, (a, b) in enumerate(pairs)]
+    pairs = ((ddv, dd_out), (dqv, dq_out), (mean, loss_out))
+    outs = [pltpu.make_async_copy(a, b, sems.at[3 + i]) for i, (a, b) in enumerate(pairs)]
+    for copy in ins:
+        copy.start()
+    for i in range(3):
+        ins[i].wait()
+        if i == 2:
+            mean[...] = lossv[:, 0:1]
+        outs[i].start()
+    for copy in outs:
         copy.wait()
 
 
@@ -399,7 +417,7 @@
             jax.ShapeDtypeStruct(queries.shape, BF),
             jax.ShapeDtypeStruct(documents.shape, BF),
         ],
-        in_specs=[anywhere, anywhere, pl.BlockSpec(memory_space=pltpu.SMEM)],
+        in_specs=[anywhere] * 3,
         out_specs=[anywhere] * 3,
         scratch_shapes=[
             vm((X, Y, QD, main), BF),
@@ -428,14 +446,32 @@
             vm((1, n_query), F32),
             vm(queries.shape, BF),
             vm(documents.shape, BF),
+            pltpu.SMEM((QD,), jnp.int32),
             vm((16384, 128), F32),
-            dma((54,)),
+            dma((53,)),
             dma,
-            dma((3,)),
+            dma((4,)),
         ],
         compiler_params=pltpu.CompilerParams(collective_id=0, has_side_effects=True),
     )(queries, documents, positive)
-    return (loss[0, 0], dq, dd)
+    loss, dq, dd = pl.pallas_call(
+        finish,
+        out_shape=[
+            jax.ShapeDtypeStruct((1, 1), F32),
+            jax.ShapeDtypeStruct(queries.shape, BF),
+            jax.ShapeDtypeStruct(documents.shape, BF),
+        ],
+        in_specs=[anywhere] * 3,
+        out_specs=[anywhere] * 3,
+        scratch_shapes=[
+            vm((1, n_query), F32),
+            vm(queries.shape, BF),
+            vm(documents.shape, BF),
+            vm((1, 1), F32),
+            dma((6,)),
+        ],
+    )(loss, dq, dd)
+    return (loss.reshape(()), dq, dd)
 
 
 def solution(mesh):

time: 56.2 us -> 51.5 us (0.916)
  the two profiles are of different devices: /device:TPU:16 before, /device:TPU:1 now
where the time goes in v3:
time: 51.5 us; the launch traced here: 50.9 us
  Pallas kernels  50.2 us (97%)
  between operations  0.64 us (1%)
    pallas_call x1, Pallas kernels, shards(): pl.pallas_call(kernel, out_shape=[jax.ShapeDtypeStruct((1, n_query), F32)...  48.7 us
    pallas_call x1, Pallas kernels, shards(): pl.pallas_call(finish, out_shape=[jax.ShapeDtypeStruct((1, 1), F32), jax....  1.53 us

profile of v3, /device:TPU:1, one launch (start us, length us, event | category | flops | bytes accessed | tf_op | source)
XLA Modules:
  0.0 50.9 jit_solution(11179646259927900736)
XLA Ops:
  0.6 48.7 %shard_map.58 = (f32[1,128]{1,0:T(1,128)}, bf16[4,4096]{1,0:T(4,128)(2,1)}, bf16[8,4096]{1,0:T(8,128)(2,1)}) custom-call(bf16[4,4096]{1,0:T(4,128)(2,1)} %q_ref.1, bf16[8,4096]{1,0:T(8,128)(2,1)} %d_ref.1, s32[4]{0:T(128)} %p_ref.1), custom_call_target="tpu_custom_call" | custom-call | tf_op jit(solution)/shard_map/pallas_call | solution.py:413
  49.3 1.5 %shard_map.59 = (f32[1,1]{1,0:T(1,128)}, bf16[4,4096]{1,0:T(4,128)(2,1)}, bf16[8,4096]{1,0:T(8,128)(2,1)}) custom-call(f32[1,128]{1,0:T(1,128)} %get-tuple-element.9.loss_ref, bf16[4,4096]{1,0:T(4,128)(2,1)} %get-tuple-element.10.dq_ref, bf16[8,4096]{1,0:T(8,128)(2,1)} %get-tuple-element.11.dd_ref), custom_call_target="tpu_custom_call" | custom-call | tf_op jit(solution)/shard_map/pallas_call | solution.py:457
